TPU v7x, 32 devices: a whole 2x2x4 slice. The times are simulated.
32 devices in a mesh: gx: 8 (over z, y), gy: 4 (over x, core).
Axes of the slice: x: 2, y: 2, z: 4, core: 2. Of those that a mesh axis runs over, the one named last changes fastest.
Arguments:
- velocity: float32 [3, 64, 256, 384], P(None, 'gx', 'gy')
- target_profile: float32 [2, 384], replicated, may hold values from 0.5 to 1.5
- disc_turbine: int32 [32, 4], P(('gx', 'gy')), may hold values from -1 to 99, as said below
- disc_start: int32 [3, 32, 4], P(None, ('gx', 'gy')), may hold values from 0 to 256, as said below
- disc_weight: float32 [32, 4, 16, 128], P(('gx', 'gy')), may hold values from 0.2 to 1
- turbine_owner: int32 [100], replicated, may hold values from 0 to 31, as said below
- mode_flag: int32 [100], replicated, may hold values from 0 to 2
- controller_state: float32 [32, 4], P(('gx', 'gy')), may hold values from -4 to 4
Outputs:
- advanced_velocity: float32 [3, 64, 256, 384], P(None, 'gx', 'gy')
- profiles: float32 [4, 384], replicated
- thrust_setpoint: float32 [100], replicated
- controller_next: float32 [32, 4], P(('gx', 'gy'))
Inputs may be any that keep to these rules, and one draw needn't show every extreme that they name: `disc_turbine`: -1 marks an empty slot; every turbine number appears in at least one slot; some device has all 4 slots filled. `disc_start`: row 0 is a cell of the device's block along the first dimension, 0 to 7; row 1 the first of 16 cells along the second, 0 to 48; row 2 the first of 128 heights, 0 to 256. `turbine_owner`: no device owns more than 4 turbines, and some device owns exactly 4.
All inputs are finite; a program needn't handle non-finite values.
Results may differ from a plain program's by a relative error of at most 0.00013.
Values sent between devices are 32-bit elements; how exact they have to be, the bound alone decides.
A program may use at most 128 MiB of HBM per device.

v0:
```python
import jax
import jax.numpy as jnp
from jax import lax
from jax.sharding import PartitionSpec as P

STEPS = 4


VISCOSITY = 0.1
TIME_STEP = 0.2
RELAX_TIME = 2.0
CONTROL_STEP = 0.5
GAIN_PROPORTIONAL = 2.0
GAIN_INTEGRAL = 1.0
HIGHEST = lax.Precision.HIGHEST


def with_halo(cells, sides, width):
    for axis, dim in sides:
        count = lax.axis_size(axis)
        head = lax.slice_in_dim(cells, 0, width, axis=dim)
        tail = lax.slice_in_dim(cells, cells.shape[dim] - width, cells.shape[dim], axis=dim)
        cells = jnp.concatenate(
            [
                lax.ppermute(tail, axis, [(i, (i + 1) % count) for i in range(count)]),
                cells,
                lax.ppermute(head, axis, [((i + 1) % count, i) for i in range(count)]),
            ],
            axis=dim,
        )
    return cells


def pad_height(block):
    return jnp.pad(block, ((0, 0), (0, 0), (0, 0), (2, 2)))


def tendency(block):
    length_x = block.shape[1] - 4
    length_y = block.shape[2] - 4
    length_z = block.shape[3] - 4

    def shifted(offset_x, offset_y, offset_z):
        return block[
            :,
            2 + offset_x : 2 + offset_x + length_x,
            2 + offset_y : 2 + offset_y + length_y,
            2 + offset_z : 2 + offset_z + length_z,
        ]

    centre = shifted(0, 0, 0)
    grad_x = (
        8.0 * (shifted(1, 0, 0) - shifted(-1, 0, 0)) - (shifted(2, 0, 0) - shifted(-2, 0, 0))
    ) / 12.0
    grad_y = (
        8.0 * (shifted(0, 1, 0) - shifted(0, -1, 0)) - (shifted(0, 2, 0) - shifted(0, -2, 0))
    ) / 12.0
    grad_z = (
        8.0 * (shifted(0, 0, 1) - shifted(0, 0, -1)) - (shifted(0, 0, 2) - shifted(0, 0, -2))
    ) / 12.0
    laplacian = (
        shifted(1, 0, 0)
        + shifted(-1, 0, 0)
        + (shifted(0, 1, 0) + shifted(0, -1, 0))
        + (shifted(0, 0, 1) + shifted(0, 0, -1))
        - 6.0 * centre
    )
    advection = centre[0:1] * grad_x + centre[1:2] * grad_y + centre[2:3] * grad_z
    return VISCOSITY * laplacian - advection


def control_terms(mode_flag):
    rated_speed = jnp.where(mode_flag == 0, 0.7, jnp.where(mode_flag == 1, 0.9, 1.1)).astype(
        jnp.float32
    )
    bias_terms = jnp.where(mode_flag == 0, 1.0, jnp.where(mode_flag == 1, 0.0, -1.0)).astype(
        jnp.float32
    )
    return (rated_speed, bias_terms)


def owner_rank(turbine_owner):
    turbines = turbine_owner.shape[0]
    same_owner = turbine_owner[:, None] == turbine_owner[None, :]
    earlier = (
        jnp.arange(turbines, dtype=jnp.int32)[None, :]
        < jnp.arange(turbines, dtype=jnp.int32)[:, None]
    )
    return jnp.sum((same_owner & earlier).astype(jnp.int32), axis=1)


def thrust_from(bias_terms, speed_error, integral):
    return 0.1 + 0.9 * jax.nn.sigmoid(
        bias_terms - GAIN_PROPORTIONAL * speed_error - GAIN_INTEGRAL * integral
    )


def local(
    velocity,
    target_profile,
    disc_turbine,
    disc_start,
    disc_weight,
    turbine_owner,
    mode_flag,
    controller_state,
):
    blocks_x = lax.axis_size("gx")
    blocks_y = lax.axis_size("gy")
    devices = blocks_x * blocks_y
    device_me = lax.axis_index("gx") * blocks_y + lax.axis_index("gy")
    length_x = velocity.shape[1]
    length_y = velocity.shape[2]
    length_z = velocity.shape[3]
    turbines = mode_flag.shape[0]
    owned = controller_state.shape[1]
    slots = disc_turbine.shape[1]
    tile_y = disc_weight.shape[2]
    tile_z = disc_weight.shape[3]
    weights_local = disc_weight[0]
    start_x = disc_start[0, 0]
    start_y = disc_start[1, 0]
    start_z = disc_start[2, 0]
    turbine_ids = jnp.arange(turbines, dtype=jnp.int32)
    slot_onehot = (disc_turbine[0][:, None] == turbine_ids[None, :]).astype(jnp.float32)
    area_part = jnp.dot(jnp.sum(weights_local, axis=(1, 2)), slot_onehot, precision=HIGHEST)
    disc_area = lax.psum(area_part, ("gx", "gy"))
    owner_slot = owner_rank(turbine_owner)
    owner_column = turbine_owner * owned + owner_slot
    pick_table = (
        owner_column[:, None] == jnp.arange(devices * owned, dtype=jnp.int32)[None, :]
    ).astype(jnp.float32)
    mine_table = (
        (turbine_owner[:, None] == device_me)
        & (owner_slot[:, None] == jnp.arange(owned, dtype=jnp.int32)[None, :])
    ).astype(jnp.float32)
    live_slot = jnp.sum(mine_table, axis=0)
    rated_speed, bias_terms = control_terms(mode_flag)
    integral = controller_state[0]
    state_all = lax.all_gather(controller_state[0], ("gx", "gy"), axis=0, tiled=True)
    integral_all = jnp.dot(pick_table, state_all, precision=HIGHEST)
    plane_cells = float(length_x * blocks_x * length_y * blocks_y)
    profiles = jnp.zeros((4, length_z), jnp.float32)
    thrust = jnp.zeros((turbines,), jnp.float32)
    for turn_index in range(STEPS):
        streamwise = velocity[0]
        contribution = jnp.stack(
            [
                jnp.sum(
                    weights_local[slot_index]
                    * lax.dynamic_slice(
                        streamwise,
                        (start_x[slot_index], start_y[slot_index], start_z[slot_index]),
                        (1, tile_y, tile_z),
                    )[0]
                )
                for slot_index in range(slots)
            ]
        )
        numerator_part = jnp.dot(contribution, slot_onehot, precision=HIGHEST)
        plane_part = jnp.stack(
            [
                jnp.sum(velocity[0], axis=(0, 1)),
                jnp.sum(velocity[1], axis=(0, 1)),
                jnp.sum(velocity[2], axis=(0, 1)),
                jnp.sum(velocity[0] * velocity[2], axis=(0, 1)),
            ]
        )
        plane_sums, numerator = lax.psum((plane_part, numerator_part), ("gx", "gy"))
        disc_speed = numerator / disc_area
        speed_error = disc_speed - rated_speed
        integral_all = integral_all + CONTROL_STEP * speed_error
        thrust = thrust_from(bias_terms, speed_error, integral_all)
        thrust_factor = 0.5 * thrust * disc_speed * jnp.abs(disc_speed)
        slot_factor = jnp.dot(slot_onehot, thrust_factor, precision=HIGHEST)
        force_field = jnp.zeros((length_x, length_y, length_z), jnp.float32)
        for slot_index in range(slots):
            corner = (start_x[slot_index], start_y[slot_index], start_z[slot_index])
            previous = lax.dynamic_slice(force_field, corner, (1, tile_y, tile_z))
            force_field = lax.dynamic_update_slice(
                force_field,
                previous - slot_factor[slot_index] * weights_local[slot_index][None],
                corner,
            )
        plane_means = plane_sums / plane_cells
        profiles = profiles + jnp.stack(
            [
                plane_means[0],
                plane_means[1],
                plane_means[2],
                plane_means[3] - plane_means[0] * plane_means[2],
            ]
        )
        nudging = (target_profile - plane_means[0:2]) / RELAX_TIME
        padded = with_halo(velocity, (("gx", 1), ("gy", 2)), 2)
        changes = tendency(pad_height(padded))
        velocity = jnp.stack(
            [
                velocity[0] + TIME_STEP * (changes[0] + nudging[0][None, None, :] + force_field),
                velocity[1] + TIME_STEP * (changes[1] + nudging[1][None, None, :]),
                velocity[2] + TIME_STEP * changes[2],
            ]
        )
    integral = jnp.dot(integral_all, mine_table, precision=HIGHEST) + (1.0 - live_slot) * integral
    return (velocity, profiles / STEPS, thrust, integral[None, :])


def solution(mesh):
    placed = (
        P(None, "gx", "gy", None),
        P(),
        P(("gx", "gy"), None),
        P(None, ("gx", "gy"), None),
        P(("gx", "gy"), None, None, None),
        P(),
        P(),
        P(("gx", "gy"), None),
    )
    return jax.shard_map(
        local,
        mesh=mesh,
        in_specs=placed,
        out_specs=(P(None, "gx", "gy", None), P(), P(), P(("gx", "gy"), None)),
        check_vma=False,
    )
```

profile of v0, /device:TPU:0, one launch (start us, length us, event | category | flops | bytes accessed | tf_op | source)
XLA Modules:
  0.0 428.4 jit_solution(238515373934112473)
XLA Ops:
  0.6 2.5 fusion.239
  3.2 3.0 collective-permute-start.1
  6.1 3.0 collective-permute-start
  9.2 1.5 fusion.70
  36.0 2.7 convolution_bitcast_fusion.9
  38.7 38.0 %all-reduce.8 = (f32[4,384]{1,0:T(4,128)S(1)}, f32[100]{0:T(128)S(1)}, f32[100]{0:T(128)S(1)}, f32[128]{0:T(128)S(1)}) all-reduce(f32[4,384]{1,0:T(4,128)S(1)} %pad_maximum_fusion.27, f32[100]{0:T(128)S(1)} %convolution_bitcast_fusion.9, f32[100]{0:T(128)S(1)} %convolution_bitcast_fusion.8, ...), channel_id=1, replica_groups=mesh['gx'=8,'gy'=4] {'gx','gy'}, use_global_device_ids=true, to_apply=%region_4.5 | all-reduce | flops 1864 | bytes 14912 | tf_op jit(solution)/shard_map/psum | solution.py:169
  87.5 1.6 constant_dynamic-update-slice_fusion
  90.4 2.3 collective-permute-done.2
  92.7 2.8 collective-permute-done.3
  95.6 2.7 select_maximum_fusion.18
  98.2 7.7 %fusion.33 = f32[3,8,64,384]{3,2,1,0:T(8,128)S(1)} fusion(f32[3,12,68,388]{3,2,1,0:T(8,128)S(1)} %select_maximum_fusion.18, f32[3,12,64,384]{3,2,1,0:T(8,128)S(1)} %get-tuple-element.121, f32[3,12,2,384]{3,2,1,0:T(2,128)S(1)} %collective-permute-done.3, f32[3,12,2,384]{3,2,1,0:T(2,128)S(1)} %collective-permute-done.2, f32[3,10,64,384]{3,2,1,0:T(8,128)} %copy-done.12, ...), kind=kLoop, calls=%fused_computation.81 | loop fusion | flops 17694720 | bytes 29712384 | tf_op jit(solution)/shard_map/sub | solution.py:69
  106.0 1.9 multiply_bitcast_fusion.5
  110.6 2.7 convolution_bitcast_fusion.6
  113.4 39.6 %all-reduce.7 = (f32[4,384]{1,0:T(4,128)S(1)}, f32[100]{0:T(128)S(1)}) all-reduce(f32[4,384]{1,0:T(4,128)S(1)} %pad_maximum_fusion.28, f32[100]{0:T(128)S(1)} %convolution_bitcast_fusion.6), channel_id=1, replica_groups=mesh['gx'=8,'gy'=4] {'gx','gy'}, use_global_device_ids=true, to_apply=%region_17.18 | all-reduce | flops 1636 | bytes 13088 | tf_op jit(solution)/shard_map/psum | solution.py:169
  153.0 1.6 pad_maximum_fusion.8
  155.7 3.7 collective-permute-start.4
  161.8 2.7 dynamic_update_slice.52
  164.6 1.5 bitcast_subtract_fusion.8
  166.1 2.7 dynamic_update_slice.53
  168.8 1.4 bitcast_subtract_fusion.7
  170.3 1.6 dynamic_update_slice.54
  171.9 1.5 bitcast_subtract_fusion.6
  173.4 2.8 dynamic_update_slice.55
  176.2 7.1 %collective-permute-done.4 = f32[3,2,64,384]{3,2,1,0:T(8,128)} collective-permute-done((f32[3,2,64,384]{3,2,1,0:T(8,128)}, f32[3,2,64,384]{3,2,1,0:T(8,128)}, u32[]{:S(2)}, u32[]{:S(2)}) %collective-permute-start.4) | collective-permute-done | bytes 589856 | tf_op jit(solution)/shard_map/ppermute | solution.py:27
  185.4 3.9 pad_maximum_fusion.3
  190.4 7.7 %select_maximum_fusion.12 = f32[3,12,68,388]{3,2,1,0:T(8,128)S(1)} fusion(f32[3,12,2,384]{3,2,1,0:T(2,128)S(1)} %collective-permute-done.6, f32[3,12,2,384]{3,2,1,0:T(2,128)S(1)} %collective-permute-done.7, f32[3,2,64,384]{3,2,1,0:T(8,128)} %collective-permute-done.4, f32[3,2,64,384]{3,2,1,0:T(8,128)} %collective-permute-done.5, ...), kind=kLoop, calls=%fused_computation.14 | loop fusion | flops 15197184 | bytes 7559424 | tf_op jit(solution)/shard_map/concatenate | solution.py:23
  198.2 5.6 %pad_maximum_fusion = (f32[3,12,66,384]{3,2,1,0:T(8,128)}, f32[3,12,66,384]{3,2,1,0:T(8,128)}) fusion(f32[3,12,2,384]{3,2,1,0:T(2,128)S(1)} %collective-permute-done.6, f32[3,2,64,384]{3,2,1,0:T(8,128)} %collective-permute-done.4, f32[1,8,64,384]{3,2,1,0:T(8,128)S(1)} %copy-done.7, f32[1,8,64,384]{3,2,1,0:T(8,128)S(1)} %copy-done.6, ...), kind=kLoop, calls=%fused_computation.27 | loop fusion | flops 9123840 | bytes 11059200 | tf_op jit(solution)/shard_map/concatenate | solution.py:23
  203.8 9.0 %fusion.24 = f32[3,8,64,384]{3,2,1,0:T(8,128)S(1)} fusion(f32[3,12,68,388]{3,2,1,0:T(8,128)S(1)} %select_maximum_fusion.12, f32[3,12,66,384]{3,2,1,0:T(8,128)} %get-tuple-element.86, f32[3,12,66,384]{3,2,1,0:T(8,128)} %get-tuple-element.85, f32[3,10,64,384]{3,2,1,0:T(8,128)} %get-tuple-element.107, f32[3,10,64,384]{3,2,1,0:T(8,128)} %get-tuple-element.106, ...), kind=kLoop, calls=%fused_computation.69 | loop fusion | flops 16515072 | bytes 35389440 | tf_op jit(solution)/shard_map/sub | solution.py:69
  212.8 1.9 multiply_bitcast_fusion.3
  216.2 2.6 fusion.226
  219.5 2.8 convolution_bitcast_fusion.4
  222.3 39.0 %all-reduce.6 = (f32[4,384]{1,0:T(4,128)S(1)}, f32[100]{0:T(128)S(1)}) all-reduce(f32[4,384]{1,0:T(4,128)S(1)} %pad_maximum_fusion.29, f32[100]{0:T(128)S(1)} %convolution_bitcast_fusion.4), channel_id=1, replica_groups=mesh['gx'=8,'gy'=4] {'gx','gy'}, use_global_device_ids=true, to_apply=%region_27.28 | all-reduce | flops 1636 | bytes 13088 | tf_op jit(solution)/shard_map/psum | solution.py:169
  261.3 1.6 pad_maximum_fusion.9
  264.0 3.6 collective-permute-start.8
  270.0 2.7 dynamic_update_slice.56
  272.8 1.5 bitcast_subtract_fusion.5
  274.3 2.7 dynamic_update_slice.57
  278.4 1.6 dynamic_update_slice.58
  280.1 1.5 bitcast_subtract_fusion.3
  281.6 2.8 dynamic_update_slice.59
  284.4 7.1 %collective-permute-done.8 = f32[3,2,64,384]{3,2,1,0:T(8,128)S(1)} collective-permute-done((f32[3,2,64,384]{3,2,1,0:T(8,128)}, f32[3,2,64,384]{3,2,1,0:T(8,128)S(1)}, u32[]{:S(2)}, u32[]{:S(2)}) %collective-permute-start.8) | collective-permute-done | bytes 589856 | tf_op jit(solution)/shard_map/ppermute | solution.py:27
  293.3 2.9 pad_maximum_fusion.4
  296.2 2.2 collective-permute-done.11
  298.4 7.7 %select_maximum_fusion.6 = f32[3,12,68,388]{3,2,1,0:T(8,128)S(1)} fusion(f32[3,12,2,384]{3,2,1,0:T(2,128)S(1)} %collective-permute-done.10, f32[3,12,2,384]{3,2,1,0:T(2,128)S(1)} %collective-permute-done.11, f32[3,2,64,384]{3,2,1,0:T(8,128)S(1)} %collective-permute-done.8, f32[3,2,64,384]{3,2,1,0:T(8,128)} %collective-permute-done.9, ...), kind=kLoop, calls=%fused_computation.8 | loop fusion | flops 15197184 | bytes 7559424 | tf_op jit(solution)/shard_map/concatenate | solution.py:23
  306.1 4.9 %pad_maximum_fusion.1 = (f32[3,12,66,384]{3,2,1,0:T(8,128)}, f32[3,12,66,384]{3,2,1,0:T(8,128)}) fusion(f32[3,12,2,384]{3,2,1,0:T(2,128)S(1)} %collective-permute-done.10, f32[3,2,64,384]{3,2,1,0:T(8,128)S(1)} %collective-permute-done.8, f32[1,8,64,384]{3,2,1,0:T(8,128)S(1)} %copy-done.4, f32[1,8,64,384]{3,2,1,0:T(8,128)S(1)} %copy-done.3, ...), kind=kLoop, calls=%fused_computation.29 | loop fusion | flops 9123840 | bytes 11059200 | tf_op jit(solution)/shard_map/concatenate | solution.py:23
  311.0 8.6 %fusion.15 = f32[3,8,64,384]{3,2,1,0:T(8,128)} fusion(f32[3,12,68,388]{3,2,1,0:T(8,128)S(1)} %select_maximum_fusion.6, f32[3,12,66,384]{3,2,1,0:T(8,128)} %get-tuple-element.82, f32[3,12,66,384]{3,2,1,0:T(8,128)} %get-tuple-element.81, f32[3,10,64,384]{3,2,1,0:T(8,128)} %get-tuple-element.101, f32[3,10,64,384]{3,2,1,0:T(8,128)S(1)} %get-tuple-element.100, ...), kind=kLoop, calls=%fused_computation.57 | loop fusion | flops 16515072 | bytes 35389440 | tf_op jit(solution)/shard_map/sub | solution.py:69
  319.6 3.1 multiply_bitcast_fusion.1
  322.8 1.8 fusion.74
  325.3 2.8 convolution_bitcast_fusion.2
  328.1 40.6 %all-reduce.5 = (f32[4,384]{1,0:T(4,128)S(1)}, f32[100]{0:T(128)S(1)}) all-reduce(f32[4,384]{1,0:T(4,128)S(1)} %pad_maximum_fusion.30, f32[100]{0:T(128)S(1)} %convolution_bitcast_fusion.2), channel_id=1, replica_groups=mesh['gx'=8,'gy'=4] {'gx','gy'}, use_global_device_ids=true, to_apply=%region_37.38 | all-reduce | flops 1636 | bytes 13088 | tf_op jit(solution)/shard_map/psum | solution.py:169
  370.1 3.3 collective-permute-start.12
  375.9 2.7 dynamic_update_slice.60
  380.0 2.8 dynamic_update_slice.61
  384.2 1.6 dynamic_update_slice.62
  385.9 1.5 bitcast_subtract_fusion
  387.3 2.7 dynamic_update_slice.63
  392.3 4.9 %collective-permute-done.12 = f32[3,2,64,384]{3,2,1,0:T(8,128)S(1)} collective-permute-done((f32[3,2,64,384]{3,2,1,0:T(8,128)}, f32[3,2,64,384]{3,2,1,0:T(8,128)S(1)}, u32[]{:S(2)}, u32[]{:S(2)}) %collective-permute-start.12) | collective-permute-done | bytes 589856 | tf_op jit(solution)/shard_map/ppermute | solution.py:27
  399.2 1.5 pad_maximum_fusion.5
  400.7 1.8 collective-permute-done.14
  403.8 7.7 %select_maximum_fusion = f32[3,12,68,388]{3,2,1,0:T(8,128)S(1)} fusion(f32[3,12,2,384]{3,2,1,0:T(2,128)S(1)} %collective-permute-done.14, f32[3,12,2,384]{3,2,1,0:T(2,128)S(1)} %collective-permute-done.15, f32[3,2,64,384]{3,2,1,0:T(8,128)S(1)} %collective-permute-done.12, f32[3,2,64,384]{3,2,1,0:T(8,128)} %collective-permute-done.13, ...), kind=kLoop, calls=%fused_computation.2 | loop fusion | flops 15197184 | bytes 7559424 | tf_op jit(solution)/shard_map/concatenate | solution.py:23
  411.4 4.8 %pad_maximum_fusion.2 = (f32[3,12,66,384]{3,2,1,0:T(8,128)}, f32[3,12,66,384]{3,2,1,0:T(8,128)}) fusion(f32[3,12,2,384]{3,2,1,0:T(2,128)S(1)} %collective-permute-done.14, f32[3,2,64,384]{3,2,1,0:T(8,128)S(1)} %collective-permute-done.12, f32[1,8,64,384]{3,2,1,0:T(8,128)S(1)} %get-tuple-element.98, f32[1,8,64,384]{3,2,1,0:T(8,128)S(1)} %get-tuple-element.55, ...), kind=kLoop, calls=%fused_computation.31 | loop fusion | flops 9123840 | bytes 11059200 | tf_op jit(solution)/shard_map/concatenate | solution.py:23
  416.3 7.5 %fusion.6 = f32[3,8,64,384]{3,2,1,0:T(8,128)} fusion(f32[3,12,68,388]{3,2,1,0:T(8,128)S(1)} %select_maximum_fusion, f32[3,12,66,384]{3,2,1,0:T(8,128)} %get-tuple-element.78, f32[3,12,66,384]{3,2,1,0:T(8,128)} %get-tuple-element.77, f32[3,10,64,384]{3,2,1,0:T(8,128)S(1)} %get-tuple-element.94, f32[3,10,64,384]{3,2,1,0:T(8,128)S(1)} %get-tuple-element.93, ...), kind=kLoop, calls=%fused_computation.45 | loop fusion | flops 16515072 | bytes 35389440 | tf_op jit(solution)/shard_map/sub | solution.py:69
  423.8 1.7 fusion.45
  426.8 1.6 pad_maximum_fusion.11
  (182 shorter events, 47.2 us)
Async XLA Ops:
  0.6 8.6 %copy-start = (f32[3,8,64,384]{3,2,1,0:T(8,128)S(1)}, f32[3,8,64,384]{3,2,1,0:T(8,128)}, u32[]{:S(2)}) copy-start(f32[3,8,64,384]{3,2,1,0:T(8,128)} %param.8) | copy-start | bytes 7077892
  3.2 82.3 %collective-permute-start.1 = (f32[3,2,64,384]{3,2,1,0:T(8,128)}, f32[3,2,64,384]{3,2,1,0:T(8,128)}, u32[]{:S(2)}, u32[]{:S(2)}) collective-permute-start(f32[3,2,64,384]{3,2,1,0:T(8,128)} %get-tuple-element.119), channel_id=1, source_target_pairs={{0,4},{4,8},{8,12},{12,16},{16,20},{20,24},{24,28},{28,0},{1,5},{5... | collective-permute-start | bytes 1769480 | tf_op jit(solution)/shard_map/ppermute | solution.py:25
  6.1 81.4 %collective-permute-start = (f32[3,2,64,384]{3,2,1,0:T(8,128)}, f32[3,2,64,384]{3,2,1,0:T(8,128)}, u32[]{:S(2)}, u32[]{:S(2)}) collective-permute-start(f32[3,2,64,384]{3,2,1,0:T(8,128)} %get-tuple-element.118), channel_id=1, source_target_pairs={{4,0},{8,4},{12,8},{16,12},{20,16},{24,20},{28,24},{0,28},{5,1},{9... | collective-permute-start | bytes 1769480 | tf_op jit(solution)/shard_map/ppermute | solution.py:27
  10.7 0.7 copy-start.26
  10.7 24.1 %copy-start.24 = (f32[1,4,16,128]{3,2,1,0:T(8,128)S(1)}, f32[1,4,16,128]{3,2,1,0:T(8,128)}, u32[]{:S(2)}) copy-start(f32[1,4,16,128]{3,2,1,0:T(8,128)} %param.12) | copy-start | bytes 98308
  10.7 24.3 %copy-start.30 = (s32[1,4]{1,0:T(1,128)S(1)}, s32[1,4]{1,0:T(1,128)}, u32[]{:S(2)}) copy-start(s32[1,4]{1,0:T(1,128)} %param.10) | copy-start | bytes 52
  10.7 24.5 %copy-start.31 = (f32[1,4]{1,0:T(1,128)S(1)}, f32[1,4]{1,0:T(1,128)}, u32[]{:S(2)}) copy-start(f32[1,4]{1,0:T(1,128)} %param.15) | copy-start | bytes 52
  10.7 66.1 %copy-start.29 = (s32[100]{0:T(128)S(1)}, s32[100]{0:T(128)}, u32[]{:S(2)}) copy-start(s32[100]{0:T(128)} %param.13) | copy-start | bytes 1204
  10.7 66.3 %copy-start.27 = (s32[100]{0:T(128)S(1)}, s32[100]{0:T(128)}, u32[]{:S(2)}) copy-start(s32[100]{0:T(128)} %param.14) | copy-start | bytes 1204
  10.7 70.6 %copy-start.25 = (f32[2,384]{1,0:T(2,128)S(1)}, f32[2,384]{1,0:T(2,128)}, u32[]{:S(2)}) copy-start(f32[2,384]{1,0:T(2,128)} %param.9) | copy-start | bytes 9220
  84.6 0.9 copy-start.17
  87.5 10.7 %copy-start.12 = (f32[3,10,64,384]{3,2,1,0:T(8,128)}, f32[3,10,64,384]{3,2,1,0:T(8,128)S(1)}, u32[]{:S(2)}) copy-start(f32[3,10,64,384]{3,2,1,0:T(8,128)S(1)} %get-tuple-element.117) | copy-start | bytes 8847364
  89.2 9.1 %copy-start.10 = (f32[3,10,64,384]{3,2,1,0:T(8,128)}, f32[3,10,64,384]{3,2,1,0:T(8,128)S(1)}, u32[]{:S(2)}) copy-start(f32[3,10,64,384]{3,2,1,0:T(8,128)S(1)} %get-tuple-element.120) | copy-start | bytes 8847364
  89.3 3.4 collective-permute-start.2
  90.3 5.3 %collective-permute-start.3 = (f32[3,12,2,384]{3,2,1,0:T(2,128)S(1)}, f32[3,12,2,384]{3,2,1,0:T(2,128)S(1)}, u32[]{:S(2)}, u32[]{:S(2)}) collective-permute-start(f32[3,12,2,384]{3,2,1,0:T(2,128)S(1)} %get-tuple-element.89), channel_id=1, source_target_pairs={{0,1},{1,2},{2,3},{3,0},{4,5},{5,6},{6,7},{7,4},{8,9},{9,10},{10,1... | collective-permute-start | bytes 331784 | tf_op jit(solution)/shard_map/ppermute | solution.py:25
  90.4 7.9 %copy-start.21 = (f32[8,64,384]{2,1,0:T(8,128)S(1)}, f32[8,64,384]{2,1,0:T(8,128)}, u32[]{:S(2)}) copy-start(f32[8,64,384]{2,1,0:T(8,128)} %get-tuple-element.112) | copy-start | bytes 2359300
  106.0 2.4 copy-start.9
  106.0 2.4 copy-start.18
  109.8 94.0 %copy-start.1 = (f32[8,64,384]{2,1,0:T(8,128)}, f32[8,64,384]{2,1,0:T(8,128)S(1)}, u32[]{:S(2)}) copy-start(f32[8,64,384]{2,1,0:T(8,128)S(1)} %get-tuple-element.73) | copy-start | bytes 2359300
  155.7 27.7 %collective-permute-start.4 = (f32[3,2,64,384]{3,2,1,0:T(8,128)}, f32[3,2,64,384]{3,2,1,0:T(8,128)}, u32[]{:S(2)}, u32[]{:S(2)}) collective-permute-start(f32[3,2,64,384]{3,2,1,0:T(8,128)} %get-tuple-element.109), channel_id=1, source_target_pairs={{4,0},{8,4},{12,8},{16,12},{20,16},{24,20},{28,24},{0,28},{5,1},{9... | collective-permute-start | bytes 1769480 | tf_op jit(solution)/shard_map/ppermute | solution.py:27
  159.4 24.1 %collective-permute-start.5 = (f32[3,2,64,384]{3,2,1,0:T(8,128)}, f32[3,2,64,384]{3,2,1,0:T(8,128)}, u32[]{:S(2)}, u32[]{:S(2)}) collective-permute-start(f32[3,2,64,384]{3,2,1,0:T(8,128)} %get-tuple-element.108), channel_id=1, source_target_pairs={{0,4},{4,8},{8,12},{12,16},{16,20},{20,24},{24,28},{28,0},{1,5},{5... | collective-permute-start | bytes 1769480 | tf_op jit(solution)/shard_map/ppermute | solution.py:25
  176.2 9.2 %copy-start.6 = (f32[1,8,64,384]{3,2,1,0:T(8,128)S(1)}, f32[1,8,64,384]{3,2,1,0:T(8,128)}, u32[]{:S(2)}) copy-start(f32[1,8,64,384]{3,2,1,0:T(8,128)} %get-tuple-element.68) | copy-start | bytes 2359300
  176.2 9.2 %copy-start.7 = (f32[1,8,64,384]{3,2,1,0:T(8,128)S(1)}, f32[1,8,64,384]{3,2,1,0:T(8,128)}, u32[]{:S(2)}) copy-start(f32[1,8,64,384]{3,2,1,0:T(8,128)} %get-tuple-element.76) | copy-start | bytes 2359300
  184.8 4.5 %collective-permute-start.6 = (f32[3,12,2,384]{3,2,1,0:T(2,128)S(1)}, f32[3,12,2,384]{3,2,1,0:T(2,128)S(1)}, u32[]{:S(2)}, u32[]{:S(2)}) collective-permute-start(f32[3,12,2,384]{3,2,1,0:T(2,128)S(1)} %get-tuple-element.88), channel_id=1, source_target_pairs={{1,0},{2,1},{3,2},{0,3},{5,4},{6,5},{7,6},{4,7},{9,8},{10,9},{11,1... | collective-permute-start | bytes 331784 | tf_op jit(solution)/shard_map/ppermute | solution.py:27
  185.1 5.4 %collective-permute-start.7 = (f32[3,12,2,384]{3,2,1,0:T(2,128)S(1)}, f32[3,12,2,384]{3,2,1,0:T(2,128)S(1)}, u32[]{:S(2)}, u32[]{:S(2)}) collective-permute-start(f32[3,12,2,384]{3,2,1,0:T(2,128)S(1)} %get-tuple-element.87), channel_id=1, source_target_pairs={{0,1},{1,2},{2,3},{3,0},{4,5},{5,6},{6,7},{7,4},{8,9},{9,10},{10,1... | collective-permute-start | bytes 331784 | tf_op jit(solution)/shard_map/ppermute | solution.py:25
  198.2 5.6 %copy-start.23 = (f32[8,64,384]{2,1,0:T(8,128)S(1)}, f32[8,64,384]{2,1,0:T(8,128)}, u32[]{:S(2)}) copy-start(f32[8,64,384]{2,1,0:T(8,128)} %get-tuple-element.67) | copy-start | bytes 2359300
  212.8 2.7 copy-start.8
  212.8 2.7 copy-start.2
  212.8 2.7 copy-start.13
  212.8 3.3 copy-start.15
  262.9 28.9 %copy-start.3 = (f32[1,8,64,384]{3,2,1,0:T(8,128)S(1)}, f32[1,8,64,384]{3,2,1,0:T(8,128)}, u32[]{:S(2)}) copy-start(f32[1,8,64,384]{3,2,1,0:T(8,128)} %get-tuple-element.61) | copy-start | bytes 2359300
  262.9 28.9 %copy-start.4 = (f32[1,8,64,384]{3,2,1,0:T(8,128)S(1)}, f32[1,8,64,384]{3,2,1,0:T(8,128)}, u32[]{:S(2)}) copy-start(f32[1,8,64,384]{3,2,1,0:T(8,128)} %get-tuple-element.105) | copy-start | bytes 2359300
  264.0 27.5 %collective-permute-start.8 = (f32[3,2,64,384]{3,2,1,0:T(8,128)}, f32[3,2,64,384]{3,2,1,0:T(8,128)S(1)}, u32[]{:S(2)}, u32[]{:S(2)}) collective-permute-start(f32[3,2,64,384]{3,2,1,0:T(8,128)} %get-tuple-element.103), channel_id=1, source_target_pairs={{4,0},{8,4},{12,8},{16,12},{20,16},{24,20},{28,24},{0,28},{5,1},{9... | collective-permute-start | bytes 1769480 | tf_op jit(solution)/shard_map/ppermute | solution.py:27
  267.6 24.2 %collective-permute-start.9 = (f32[3,2,64,384]{3,2,1,0:T(8,128)}, f32[3,2,64,384]{3,2,1,0:T(8,128)}, u32[]{:S(2)}, u32[]{:S(2)}) collective-permute-start(f32[3,2,64,384]{3,2,1,0:T(8,128)} %get-tuple-element.102), channel_id=1, source_target_pairs={{0,4},{4,8},{8,12},{12,16},{16,20},{20,24},{24,28},{28,0},{1,5},{5... | collective-permute-start | bytes 1769480 | tf_op jit(solution)/shard_map/ppermute | solution.py:25
  292.8 3.4 collective-permute-start.10
  293.2 5.1 %collective-permute-start.11 = (f32[3,12,2,384]{3,2,1,0:T(2,128)S(1)}, f32[3,12,2,384]{3,2,1,0:T(2,128)S(1)}, u32[]{:S(2)}, u32[]{:S(2)}) collective-permute-start(f32[3,12,2,384]{3,2,1,0:T(2,128)S(1)} %get-tuple-element.83), channel_id=1, source_target_pairs={{0,1},{1,2},{2,3},{3,0},{4,5},{5,6},{6,7},{7,4},{8,9},{9,10},{10,1... | collective-permute-start | bytes 331784 | tf_op jit(solution)/shard_map/ppermute | solution.py:25
  306.1 4.9 %copy-start.22 = (f32[8,64,384]{2,1,0:T(8,128)S(1)}, f32[8,64,384]{2,1,0:T(8,128)}, u32[]{:S(2)}) copy-start(f32[8,64,384]{2,1,0:T(8,128)} %get-tuple-element.60) | copy-start | bytes 2359300
  311.0 8.6 %copy-start.5 = (f32[1,8,64,384]{3,2,1,0:T(8,128)S(1)}, f32[1,8,64,384]{3,2,1,0:T(8,128)}, u32[]{:S(2)}) copy-start(f32[1,8,64,384]{3,2,1,0:T(8,128)} %get-tuple-element.105) | copy-start | bytes 2359300
  319.6 3.2 copy-start.11
  319.6 3.2 copy-start.14
  319.6 3.2 copy-start.19
  319.6 3.2 copy-start.20
  370.1 27.1 %collective-permute-start.12 = (f32[3,2,64,384]{3,2,1,0:T(8,128)}, f32[3,2,64,384]{3,2,1,0:T(8,128)S(1)}, u32[]{:S(2)}, u32[]{:S(2)}) collective-permute-start(f32[3,2,64,384]{3,2,1,0:T(8,128)} %get-tuple-element.96), channel_id=1, source_target_pairs={{4,0},{8,4},{12,8},{16,12},{20,16},{24,20},{28,24},{0,28},{5,1},{9... | collective-permute-start | bytes 1769480 | tf_op jit(solution)/shard_map/ppermute | solution.py:27
  373.4 23.8 %collective-permute-start.13 = (f32[3,2,64,384]{3,2,1,0:T(8,128)}, f32[3,2,64,384]{3,2,1,0:T(8,128)}, u32[]{:S(2)}, u32[]{:S(2)}) collective-permute-start(f32[3,2,64,384]{3,2,1,0:T(8,128)} %get-tuple-element.95), channel_id=1, source_target_pairs={{0,4},{4,8},{8,12},{12,16},{16,20},{20,24},{24,28},{28,0},{1,5},{5... | collective-permute-start | bytes 1769480 | tf_op jit(solution)/shard_map/ppermute | solution.py:25
  373.4 24.8 %copy-start.28 = (f32[100]{0:T(128)}, f32[100]{0:T(128)S(1)}, u32[]{:S(2)}) copy-start(f32[100]{0:T(128)S(1)} %get-tuple-element.51) | copy-start | bytes 1204
  398.2 4.3 collective-permute-start.14
  399.2 4.5 %collective-permute-start.15 = (f32[3,12,2,384]{3,2,1,0:T(2,128)S(1)}, f32[3,12,2,384]{3,2,1,0:T(2,128)S(1)}, u32[]{:S(2)}, u32[]{:S(2)}) collective-permute-start(f32[3,12,2,384]{3,2,1,0:T(2,128)S(1)} %get-tuple-element.79), channel_id=1, source_target_pairs={{0,1},{1,2},{2,3},{3,0},{4,5},{5,6},{6,7},{7,4},{8,9},{9,10},{10,1... | collective-permute-start | bytes 331784 | tf_op jit(solution)/shard_map/ppermute | solution.py:25
  423.8 1.7 copy-start.16
where the time goes:
time: 432 us; the launch traced here: 428 us
  blocking collectives  157 us (36%)
  other arithmetic  131 us (30%)
  local copies, waits for them, and re-layouts  52.6 us (12%)
  waiting for transfers between devices  31.1 us (7%)
  between operations  24.1 us (6%)
  starting transfers between devices  19.8 us (5%)
  matrix products  12.8 us (3%)
    psum x4, blocking collectives, local(): plane_sums, numerator = lax.psum((plane_part, numerator_part), ('gx', 'gy'))  157 us
    concatenate x13, other arithmetic, with_halo(): jnp.concatenate([lax.ppermute(tail, axis, [(i, (i + 1) % count) for i in...  52.6 us
    dynamic_update_slice x16, local copies, waits for them, and re-layouts, local(): lax.dynamic_update_slice(force_field, previous - slot_factor[slot_index]...  33.3 us
    sub x4, other arithmetic, tendency(): return VISCOSITY * laplacian - advection  32.8 us
    ppermute x8, waiting for transfers between devices, with_halo(): lax.ppermute(head, axis, [((i + 1) % count, i) for i in range(count)])  23.2 us
    sub x16, other arithmetic, local(): previous - slot_factor[slot_index] * weights_local[slot_index][None]  17.8 us
    ppermute x8, starting transfers between devices, with_halo(): lax.ppermute(head, axis, [((i + 1) % count, i) for i in range(count)])  16.4 us
    dot_general x4, matrix products, local(): numerator_part = jnp.dot(contribution, slot_onehot, precision=HIGHEST)  11 us
  transfers between devices with their start and end apart: 16, of which 11 were waited for; matrix products, arithmetic and copies ran while one was open for 18% of the time, Pallas kernels for 0%

commit v1 on v0

v1 whole, which is shorter than its diff:
```python
import functools

import jax
import jax.numpy as jnp
from jax import lax
from jax.experimental import pallas as pl
from jax.experimental.pallas import tpu as pltpu
from jax.sharding import PartitionSpec as P

STEPS = 4

VISCOSITY = 0.1
TIME_STEP = 0.2
RELAX_TIME = 2.0
CONTROL_STEP = 0.5
GAIN_PROPORTIONAL = 2.0
GAIN_INTEGRAL = 1.0
HIGHEST = lax.Precision.HIGHEST
MESH = pl.DeviceIdType.MESH
PAD = 8
CHUNKS = 2


def kernel(
    n_gx,
    n_gy,
    vel_ref,
    target_ref,
    turbine_ref,
    start_ref,
    weight_ref,
    owner_ref,
    mode_ref,
    state_ref,
    out_ref,
    prof_ref,
    thrust_ref,
    next_ref,
    buf,
    dense,
    acc,
    acc_disc,
    pay,
    gather_y,
    gather_x,
    send_x,
    recv_x,
    send_y,
    recv_y,
    load_sem,
    send_1,
    recv_1,
    send_2,
    recv_2,
    integral_ref,
    area_ref,
    factor_ref,
    mine_ref,
    nudge_ref,
):
    len_x, len_y, len_z = vel_ref.shape[1:]
    slots, tile_y, tile_z = weight_ref.shape[1:]
    owned = state_ref.shape[1]
    turbines = owner_ref.shape[1]
    gx = lax.axis_index("gx")
    gy = lax.axis_index("gy")
    right_x = (lax.rem(gx + 1, n_gx), gy)
    left_x = (lax.rem(gx + n_gx - 1, n_gx), gy)
    right_y = (gx, lax.rem(gy + 1, n_gy))
    left_y = (gx, lax.rem(gy + n_gy - 1, n_gy))
    rows = len_y // CHUNKS

    barrier = pltpu.get_barrier_semaphore()
    for d in range(1, n_gy):
        pl.semaphore_signal(barrier, inc=1, device_id=(gx, lax.rem(gy + d, n_gy)), device_id_type=MESH)
    for d in range(1, n_gx):
        pl.semaphore_signal(barrier, inc=1, device_id=(lax.rem(gx + d, n_gx), gy), device_id_type=MESH)

    load = pltpu.make_async_copy(
        vel_ref, buf.at[0, :, pl.ds(2, len_x), pl.ds(PAD, len_y), :], load_sem
    )
    load.start()
    pl.semaphore_wait(barrier, n_gx + n_gy - 2)

    def x_copy(parity, side, chunk, first):
        at = PAD + chunk * rows
        begin = len_x - 2 if side == 0 else 0
        if first:
            source = vel_ref.at[:, pl.ds(begin, 2), pl.ds(chunk * rows, rows), :]
        else:
            source = buf.at[parity, :, pl.ds(begin + 2, 2), pl.ds(at, rows), :]
        place = 0 if side == 0 else len_x + 2
        return pltpu.make_async_remote_copy(
            src_ref=source,
            dst_ref=buf.at[parity, :, pl.ds(place, 2), pl.ds(at, rows), :],
            send_sem=send_x.at[side, chunk],
            recv_sem=recv_x.at[parity, side, chunk],
            device_id=right_x if side == 0 else left_x,
            device_id_type=MESH,
        )

    def y_copy(parity, side, first):
        begin = len_y - PAD if side == 0 else 0
        if first:
            source = vel_ref.at[:, :, pl.ds(begin, PAD), :]
        else:
            source = buf.at[parity, :, pl.ds(2, len_x), pl.ds(PAD + begin, PAD), :]
        place = 0 if side == 0 else PAD + len_y
        return pltpu.make_async_remote_copy(
            src_ref=source,
            dst_ref=buf.at[parity, :, pl.ds(2, len_x), pl.ds(place, PAD), :],
            send_sem=send_y.at[side],
            recv_sem=recv_y.at[parity, side],
            device_id=right_y if side == 0 else left_y,
            device_id_type=MESH,
        )

    for side in range(2):
        y_copy(0, side, True).start()
    for chunk in range(CHUNKS):
        for side in range(2):
            x_copy(0, side, chunk, True).start()

    for s in range(slots):
        rows_hot = (
            lax.broadcasted_iota(jnp.int32, (len_y, tile_y), 0)
            - lax.broadcasted_iota(jnp.int32, (len_y, tile_y), 1)
            == start_ref[1, 0, s]
        ).astype(jnp.float32)
        cols_hot = (
            lax.broadcasted_iota(jnp.int32, (tile_z, len_z), 1)
            - lax.broadcasted_iota(jnp.int32, (tile_z, len_z), 0)
            == start_ref[2, 0, s]
        ).astype(jnp.float32)
        tall = jnp.dot(rows_hot, weight_ref[0, s], precision=HIGHEST, preferred_element_type=jnp.float32)
        dense[s] = jnp.dot(tall, cols_hot, precision=HIGHEST, preferred_element_type=jnp.float32)

    lane_t = lax.broadcasted_iota(jnp.int32, (1, turbines), 1)

    def hot(s):
        return (lane_t == turbine_ref[0, s]).astype(jnp.float32)

    owner = owner_ref[...]
    me = gx * n_gy + gy
    pair_row = lax.broadcasted_iota(jnp.int32, (turbines, turbines), 0)
    pair_col = lax.broadcasted_iota(jnp.int32, (turbines, turbines), 1)
    owner_f = owner.astype(jnp.float32)
    owner_column = jnp.sum(jnp.where(pair_row == pair_col, owner_f, 0.0), axis=1, keepdims=True)
    rank = jnp.sum(
        jnp.where((owner_column == owner_f) & (pair_row < pair_col), 1.0, 0.0), axis=0, keepdims=True
    )
    is_me = jnp.where(owner == me, 1.0, 0.0)
    mine_integral = jnp.zeros((1, turbines), jnp.float32)
    area = jnp.zeros((1, turbines), jnp.float32)
    for r in range(owned):
        mine_r = jnp.where(rank == float(r), is_me, 0.0)
        mine_ref[r : r + 1, :] = mine_r
        mine_integral = mine_integral + mine_r * state_ref[0, r]
    for s in range(slots):
        area = area + jnp.sum(weight_ref[0, s]) * hot(s)
    pay[...] = jnp.zeros_like(pay)
    pay[0, 5:6, 0:turbines] = area
    pay[0, 6:7, 0:turbines] = mine_integral

    mode = mode_ref[...]
    rated = jnp.where(mode == 0, 0.7, jnp.where(mode == 1, 0.9, 1.1)).astype(jnp.float32)
    bias = jnp.where(mode == 0, 1.0, jnp.where(mode == 1, 0.0, -1.0)).astype(jnp.float32)
    prof_ref[...] = jnp.zeros_like(prof_ref)

    lane = lax.broadcasted_iota(jnp.int32, (8, len_z), 1)
    keep_m1 = lane >= 1
    keep_m2 = lane >= 2
    keep_p1 = lane < len_z - 1
    keep_p2 = lane < len_z - 2

    def fold(value):
        total = value[:, 0:128]
        for z in range(128, len_z, 128):
            total = total + value[:, z : z + 128]
        return total

    def tally(x, values):
        sums = None
        discs = [None] * slots
        for group, u, v, w in values:
            terms = [u, v, w, u * w]
            sums = terms if sums is None else [a + b for a, b in zip(sums, terms)]
            for s in range(slots):
                part = dense[s, group : group + 8, :] * u
                discs[s] = part if discs[s] is None else discs[s] + part
        for c in range(4):
            acc[c] += sums[c]
        for s in range(slots):
            here = jnp.where(start_ref[0, 0, s] == x, 1.0, 0.0)
            acc_disc[s] += fold(discs[s]) * here

    def reset():
        acc[...] = jnp.zeros_like(acc)
        acc_disc[...] = jnp.zeros_like(acc_disc)

    def first_plane(x, carry):
        tally(
            x,
            [
                (g, *[buf[0, c, x + 2, PAD + g : PAD + g + 8, :] for c in range(3)])
                for g in range(0, len_y, 8)
            ],
        )
        return carry

    def update(parity, x, group):
        at = PAD + group

        def cells(c, dx, dy):
            return buf[parity, c, x + 2 + dx, at + dy : at + dy + 8, :]

        centre = [cells(c, 0, 0) for c in range(3)]
        scaled = [f * (TIME_STEP / 12.0) for f in centre]
        fresh = []
        for c in range(3):
            f = centre[c]
            xp, xm = cells(c, 1, 0), cells(c, -1, 0)
            yp, ym = cells(c, 0, 1), cells(c, 0, -1)
            zp = jnp.where(keep_p1, pltpu.roll(f, len_z - 1, 1), 0.0)
            zm = jnp.where(keep_m1, pltpu.roll(f, 1, 1), 0.0)
            zp2 = jnp.where(keep_p2, pltpu.roll(f, len_z - 2, 1), 0.0)
            zm2 = jnp.where(keep_m2, pltpu.roll(f, 2, 1), 0.0)
            grad_x = 8.0 * (xp - xm) - (cells(c, 2, 0) - cells(c, -2, 0))
            grad_y = 8.0 * (yp - ym) - (cells(c, 0, 2) - cells(c, 0, -2))
            grad_z = 8.0 * (zp - zm) - (zp2 - zm2)
            around = (xp + xm) + (yp + ym) + (zp + zm)
            advection = scaled[0] * grad_x + scaled[1] * grad_y + scaled[2] * grad_z
            fresh.append(
                (1.0 - 6.0 * TIME_STEP * VISCOSITY) * f + (TIME_STEP * VISCOSITY) * around - advection
            )
        push = nudge_ref[0]
        for s in range(slots):
            gain = jnp.where(start_ref[0, 0, s] == x, factor_ref[s], 0.0)
            push = push + gain * dense[s, group : group + 8, :]
        fresh[0] = fresh[0] + push
        fresh[1] = fresh[1] + nudge_ref[1]
        for c in range(3):
            buf[1 - parity, c, x + 2, at : at + 8, :] = fresh[c]
        return (group, *fresh)

    def sweep(parity, x, lower, upper):
        tally(x, [update(parity, x, g) for g in range(lower, upper, 8)])

    def reduce_all(parity):
        numerator = jnp.zeros((1, turbines), jnp.float32)
        for s in range(slots):
            numerator = numerator + jnp.sum(acc_disc[s]) * hot(s)
        for c in range(4):
            pay[0, c : c + 1, 0:len_z] = jnp.sum(acc[c], axis=0, keepdims=True)
        pay[0, 4:5, 0:turbines] = numerator
        copies = []
        for d in range(1, n_gy):
            copies.append(
                pltpu.make_async_remote_copy(
                    src_ref=pay.at[0],
                    dst_ref=gather_y.at[parity, gy],
                    send_sem=send_1.at[d],
                    recv_sem=recv_1.at[parity, gy],
                    device_id=(gx, lax.rem(gy + d, n_gy)),
                    device_id_type=MESH,
                )
            )
            copies[-1].start()
        gather_y[parity, gy] = pay[0]
        for d in range(1, n_gy):
            sender = lax.rem(gy + d, n_gy)
            pltpu.make_async_remote_copy(
                src_ref=pay.at[0],
                dst_ref=gather_y.at[parity, sender],
                send_sem=send_1.at[d],
                recv_sem=recv_1.at[parity, sender],
                device_id=(gx, sender),
                device_id_type=MESH,
            ).wait_recv()
        total = gather_y[parity, 0]
        for d in range(1, n_gy):
            total = total + gather_y[parity, d]
        pay[1] = total
        for d in range(1, n_gx):
            copies.append(
                pltpu.make_async_remote_copy(
                    src_ref=pay.at[1],
                    dst_ref=gather_x.at[parity, gx],
                    send_sem=send_2.at[d],
                    recv_sem=recv_2.at[parity, gx],
                    device_id=(lax.rem(gx + d, n_gx), gy),
                    device_id_type=MESH,
                )
            )
            copies[-1].start()
        gather_x[parity, gx] = total
        for d in range(1, n_gx):
            sender = lax.rem(gx + d, n_gx)
            pltpu.make_async_remote_copy(
                src_ref=pay.at[1],
                dst_ref=gather_x.at[parity, sender],
                send_sem=send_2.at[d],
                recv_sem=recv_2.at[parity, sender],
                device_id=(sender, gy),
                device_id_type=MESH,
            ).wait_recv()
        for copy in copies:
            copy.wait_send()
        total = gather_x[parity, 0]
        for d in range(1, n_gx):
            total = total + gather_x[parity, d]
        return total

    cells_total = float(len_x * n_gx * len_y * n_gy)

    def control(total, step):
        means = total[0:4, 0:len_z] * (1.0 / cells_total)
        prof_ref[0:3, :] += means[0:3] * (1.0 / STEPS)
        prof_ref[3:4, :] += (means[3:4] - means[0:1] * means[2:3]) * (1.0 / STEPS)
        nudge = (target_ref[...] - means[0:2]) * (TIME_STEP / RELAX_TIME)
        for c in range(2):
            nudge_ref[c] = jnp.broadcast_to(nudge[c : c + 1], (8, len_z))

        @pl.when(step == 0)
        def _():
            area_ref[...] = total[5:6, 0:turbines]
            integral_ref[...] = total[6:7, 0:turbines]

        speed = total[4:5, 0:turbines] / area_ref[...]
        error = speed - rated
        integral = integral_ref[...] + CONTROL_STEP * error
        integral_ref[...] = integral
        thrust = 0.1 + 0.9 * jax.nn.sigmoid(
            bias - GAIN_PROPORTIONAL * error - GAIN_INTEGRAL * integral
        )
        thrust_ref[...] = thrust
        strength = (-0.5 * TIME_STEP) * thrust * speed * jnp.abs(speed)
        for s in range(slots):
            factor_ref[s] = jnp.sum(strength * hot(s))

    reset()
    load.wait()
    lax.fori_loop(0, len_x, first_plane, 0)

    def step_body(step, carry):
        parity = lax.rem(step, 2)
        total = reduce_all(parity)
        control(total, step)
        reset()
        for side in range(2):
            y_copy(parity, side, False).wait()
        for chunk in range(CHUNKS):
            for side in range(2):
                x_copy(parity, side, chunk, False).wait()
            lower = chunk * rows

            def edge(i, carry):
                sweep(parity, i + (i // 2) * (len_x - 4), lower, lower + rows)
                return carry

            lax.fori_loop(0, 4, edge, 0)

            @pl.when(step < STEPS - 1)
            def _():
                for side in range(2):
                    x_copy(1 - parity, side, chunk, False).start()

        def inner(x, carry):
            sweep(parity, x, 0, len_y)
            return carry

        lax.fori_loop(2, len_x - 2, inner, 0)

        @pl.when(step < STEPS - 1)
        def _():
            for side in range(2):
                y_copy(1 - parity, side, False).start()

        return carry

    lax.fori_loop(0, STEPS, step_body, 0)
    store = pltpu.make_async_copy(
        buf.at[STEPS % 2, :, pl.ds(2, len_x), pl.ds(PAD, len_y), :], out_ref, load_sem
    )
    store.start()
    lane_o = lax.broadcasted_iota(jnp.int32, (1, owned), 1)
    result = jnp.zeros((1, owned), jnp.float32)
    for r in range(owned):
        mine_r = mine_ref[r : r + 1, :]
        value = jnp.sum(mine_r * integral_ref[...]) + (1.0 - jnp.sum(mine_r)) * state_ref[0, r]
        result = jnp.where(lane_o == r, value, result)
    next_ref[...] = result
    store.wait()


def local(
    n_gx,
    n_gy,
    velocity,
    target_profile,
    disc_turbine,
    disc_start,
    disc_weight,
    turbine_owner,
    mode_flag,
    controller_state,
):
    _, len_x, len_y, len_z = velocity.shape
    turbines = mode_flag.shape[0]
    slots = disc_turbine.shape[1]
    owned = controller_state.shape[1]
    wide = -(-max(len_z, turbines) // 128) * 128
    any_spec = pl.BlockSpec(memory_space=pl.ANY)
    vmem = pl.BlockSpec(memory_space=pltpu.VMEM)
    smem = pl.BlockSpec(memory_space=pltpu.SMEM)
    f32 = jnp.float32
    dma = pltpu.SemaphoreType.DMA
    out, prof, thrust, following = pl.pallas_call(
        functools.partial(kernel, n_gx, n_gy),
        out_shape=(
            jax.ShapeDtypeStruct(velocity.shape, f32),
            jax.ShapeDtypeStruct((4, len_z), f32),
            jax.ShapeDtypeStruct((1, turbines), f32),
            jax.ShapeDtypeStruct((1, owned), f32),
        ),
        in_specs=[any_spec, vmem, smem, smem, vmem, vmem, vmem, smem],
        out_specs=(any_spec, vmem, vmem, vmem),
        scratch_shapes=[
            pltpu.VMEM((2, 3, len_x + 4, len_y + 2 * PAD, len_z), f32),
            pltpu.VMEM((slots, len_y, len_z), f32),
            pltpu.VMEM((4, 8, len_z), f32),
            pltpu.VMEM((slots, 8, 128), f32),
            pltpu.VMEM((2, 8, wide), f32),
            pltpu.VMEM((2, n_gy, 8, wide), f32),
            pltpu.VMEM((2, n_gx, 8, wide), f32),
            dma((2, CHUNKS)),
            dma((2, 2, CHUNKS)),
            dma((2,)),
            dma((2, 2)),
            dma,
            dma((n_gy,)),
            dma((2, n_gy)),
            dma((n_gx,)),
            dma((2, n_gx)),
            pltpu.VMEM((1, turbines), f32),
            pltpu.VMEM((1, turbines), f32),
            pltpu.SMEM((slots,), f32),
            pltpu.VMEM((owned, turbines), f32),
            pltpu.VMEM((2, 8, len_z), f32),
        ],
        compiler_params=pltpu.CompilerParams(
            collective_id=0, has_side_effects=True, vmem_limit_bytes=48 * 1024 * 1024
        ),
    )(
        velocity,
        target_profile,
        disc_turbine,
        disc_start,
        disc_weight,
        turbine_owner[None, :],
        mode_flag[None, :],
        controller_state,
    )
    return out, prof, thrust[0], following


def solution(mesh):
    placed = (
        P(None, "gx", "gy", None),
        P(),
        P(("gx", "gy"), None),
        P(None, ("gx", "gy"), None),
        P(("gx", "gy"), None, None, None),
        P(),
        P(),
        P(("gx", "gy"), None),
    )
    return jax.shard_map(
        functools.partial(local, mesh.shape["gx"], mesh.shape["gy"]),
        mesh=mesh,
        in_specs=placed,
        out_specs=(P(None, "gx", "gy", None), P(), P(), P(("gx", "gy"), None)),
        check_vma=False,
    )
```

time: 432 us -> 143 us (0.33)
  blocking collectives: 157 us -> 0 us
  Pallas kernels: 0 us -> 133 us
  other arithmetic: 131 us -> 0 us
  local copies, waits for them, and re-layouts: 52.6 us -> 9.42 us
  waiting for transfers between devices: 31.1 us -> 0 us
  between operations: 24.1 us -> 0.66 us
  starting transfers between devices: 19.8 us -> 0 us
  matrix products: 12.8 us -> 0 us
    psum x4 -> x0, blocking collectives: 157 us -> none  [local(): plane_sums, numerator = lax.psum((plane_part, numerator_part), ('gx', 'gy'))]
    pallas_call x0 -> x1, Pallas kernels: none -> 133 us  [local(): pl.pallas_call(functools.partial(kernel, n_gx, n_gy), out_shape=(jax.Shap...]
    concatenate x13 -> x0, other arithmetic: 52.6 us -> none  [with_halo(): jnp.concatenate([lax.ppermute(tail, axis, [(i, (i + 1) % count) for i in...]
    sub x24 -> x0, other arithmetic: 50.7 us -> none  [the longest x4 32.8 us: tendency(): return VISCOSITY * laplacian - advection]
    dynamic_update_slice x16 -> x0, local copies, waits for them, and re-layouts: 33.3 us -> none  [local(): lax.dynamic_update_slice(force_field, previous - slot_factor[slot_index]...]
    ppermute x16 -> x0, waiting for transfers between devices: 31.1 us -> none  [the longest x8 23.2 us: with_halo(): lax.ppermute(head, axis, [((i + 1) % count, i) for i in range(count)])]
    ppermute x16 -> x0, starting transfers between devices: 19.8 us -> none  [the longest x8 16.4 us: with_halo(): lax.ppermute(head, axis, [((i + 1) % count, i) for i in range(count)])]
    dot_general x11 -> x0, matrix products: 12.8 us -> none  [the longest x4 11 us: local(): numerator_part = jnp.dot(contribution, slot_onehot, precision=HIGHEST)]
  transfers between devices with their start and end apart: 16 -> 0, of which waited for: 11 -> 0; matrix products, arithmetic and copies ran while one was open for 18% -> 0% of each run, Pallas kernels for 0% -> 0%
where the time goes in v1:
time: 143 us
  Pallas kernels  133 us (93%)
  local copies, waits for them, and re-layouts  9.42 us (7%)
    pallas_call x1, Pallas kernels, local(): pl.pallas_call(functools.partial(kernel, n_gx, n_gy), out_shape=(jax.Shap...  133 us
    unnamed x20, local copies, waits for them, and re-layouts  9.42 us

profile of v1, /device:TPU:0, one launch (start us, length us, event | category | flops | bytes accessed | tf_op | source)
XLA Modules:
  0.0 142.7 jit_solution(14460282414925256623)
XLA Ops:
  0.6 0.0 copy-start
  0.6 1.7 %copy-done = f32[3,8,64,384]{3,2,1,0:T(8,128)S(1)} copy-done((f32[3,8,64,384]{3,2,1,0:T(8,128)S(1)}, f32[3,8,64,384]{3,2,1,0:T(8,128)}, u32[]{:S(2)}) %copy-start) | copy-done | bytes 2359320
  2.3 0.0 copy-start.1
  2.3 0.8 copy-done.1
  3.1 0.0 copy-start.2
  3.1 0.7 copy-done.2
  3.7 0.0 copy-start.3
  3.7 0.7 copy-done.3
  4.4 0.0 copy-start.4
  4.4 0.7 copy-done.4
  5.1 0.0 copy-start.5
  5.1 0.7 copy-done.5
  5.7 0.0 copy-start.6
  5.7 0.7 copy-done.6
  6.4 0.0 copy-start.7
  6.4 0.7 copy-done.7
  7.0 132.6 %shard_map.111 = (f32[3,8,64,384]{3,2,1,0:T(8,128)S(1)}, f32[4,384]{1,0:T(4,128)S(1)}, f32[1,100]{1,0:T(1,128)S(1)}, f32[1,4]{1,0:T(1,128)S(1)}) custom-call(f32[3,8,64,384]{3,2,1,0:T(8,128)S(1)} %copy-done, f32[2,384]{1,0:T(2,128)S(1)} %copy-done.2, s32[1,4]{1,0:T(1,128)S(1)} %copy-done.4, s32[3,1,4]{2,1,0:T(1,128)S(1)} %copy-done.3, ...), custom_call_target="tpu_custom_call" | custom-call | tf_op jit(solution)/shard_map/pallas_call | solution.py:418
  139.7 1.4 copy.16
  141.1 0.6 copy.17
  141.7 0.5 copy.18
  142.2 0.5 copy.19
Async XLA Ops:
  0.6 1.7 %copy-start = (f32[3,8,64,384]{3,2,1,0:T(8,128)S(1)}, f32[3,8,64,384]{3,2,1,0:T(8,128)}, u32[]{:S(2)}) copy-start(f32[3,8,64,384]{3,2,1,0:T(8,128)} %vel_ref.1) | copy-start | bytes 7077892
  2.3 0.8 copy-start.1
  3.1 0.7 copy-start.2
  3.7 0.7 copy-start.3
  4.4 0.7 copy-start.4
  5.1 0.7 copy-start.5
  5.7 0.7 copy-start.6
  6.4 0.7 copy-start.7

commit v2 on v1

--- a/solution.py
+++ b/solution.py
@@ -18,20 +18,20 @@
 HIGHEST = lax.Precision.HIGHEST
 MESH = pl.DeviceIdType.MESH
 PAD = 8
-CHUNKS = 2
+CHUNKS = 4
 
 
 def kernel(
     n_gx,
     n_gy,
     vel_ref,
-    target_ref,
-    turbine_ref,
-    start_ref,
-    weight_ref,
-    owner_ref,
-    mode_ref,
-    state_ref,
+    target_in,
+    turbine_in,
+    start_in,
+    weight_in,
+    owner_in,
+    mode_in,
+    state_in,
     out_ref,
     prof_ref,
     thrust_ref,
@@ -57,11 +57,20 @@
     factor_ref,
     mine_ref,
     nudge_ref,
+    target_ref,
+    turbine_ref,
+    start_ref,
+    weight_ref,
+    owner_ref,
+    mode_ref,
+    state_ref,
+    small_sem,
+    store_sem,
 ):
     len_x, len_y, len_z = vel_ref.shape[1:]
-    slots, tile_y, tile_z = weight_ref.shape[1:]
-    owned = state_ref.shape[1]
-    turbines = owner_ref.shape[1]
+    slots, tile_y, tile_z = weight_in.shape[1:]
+    owned = state_in.shape[1]
+    turbines = owner_in.shape[1]
     gx = lax.axis_index("gx")
     gy = lax.axis_index("gy")
     right_x = (lax.rem(gx + 1, n_gx), gy)
@@ -79,7 +88,22 @@
     load = pltpu.make_async_copy(
         vel_ref, buf.at[0, :, pl.ds(2, len_x), pl.ds(PAD, len_y), :], load_sem
     )
-    load.start()
+    small = [
+        pltpu.make_async_copy(source, place, small_sem.at[i])
+        for i, (source, place) in enumerate(
+            [
+                (weight_in, weight_ref),
+                (start_in, start_ref),
+                (turbine_in, turbine_ref),
+                (owner_in, owner_ref),
+                (mode_in, mode_ref),
+                (state_in, state_ref),
+                (target_in, target_ref),
+            ]
+        )
+    ]
+    for copy in small:
+        copy.start()
     pl.semaphore_wait(barrier, n_gx + n_gy - 2)
 
     def x_copy(parity, side, chunk, first):
@@ -120,6 +144,9 @@
     for chunk in range(CHUNKS):
         for side in range(2):
             x_copy(0, side, chunk, True).start()
+    load.start()
+    for copy in small:
+        copy.wait()
 
     for s in range(slots):
         rows_hot = (
@@ -246,7 +273,7 @@
     def sweep(parity, x, lower, upper):
         tally(x, [update(parity, x, g) for g in range(lower, upper, 8)])
 
-    def reduce_all(parity):
+    def reduce_all(parity, step):
         numerator = jnp.zeros((1, turbines), jnp.float32)
         for s in range(slots):
             numerator = numerator + jnp.sum(acc_disc[s]) * hot(s)
@@ -293,6 +320,12 @@
                 )
             )
             copies[-1].start()
+
+        @pl.when(step > 0)
+        def _():
+            for side in range(2):
+                x_copy(parity, side, CHUNKS - 1, False).start()
+
         gather_x[parity, gx] = total
         for d in range(1, n_gx):
             sender = lax.rem(gx + d, n_gx)
@@ -342,14 +375,22 @@
     load.wait()
     lax.fori_loop(0, len_x, first_plane, 0)
 
+    def store(part):
+        begin, size = [(2, len_x - 4), (0, 2), (len_x - 2, 2)][part]
+        return pltpu.make_async_copy(
+            buf.at[STEPS % 2, :, pl.ds(2 + begin, size), pl.ds(PAD, len_y), :],
+            out_ref.at[:, pl.ds(begin, size), :, :],
+            store_sem.at[part],
+        )
+
     def step_body(step, carry):
         parity = lax.rem(step, 2)
-        total = reduce_all(parity)
+        total = reduce_all(parity, step)
         control(total, step)
         reset()
         for side in range(2):
             y_copy(parity, side, False).wait()
-        for chunk in range(CHUNKS):
+        def edges(chunk):
             for side in range(2):
                 x_copy(parity, side, chunk, False).wait()
             lower = chunk * rows
@@ -363,13 +404,21 @@
             @pl.when(step < STEPS - 1)
             def _():
                 for side in range(2):
-                    x_copy(1 - parity, side, chunk, False).start()
+                    if chunk < CHUNKS - 1:
+                        x_copy(1 - parity, side, chunk, False).start()
 
         def inner(x, carry):
             sweep(parity, x, 0, len_y)
             return carry
 
-        lax.fori_loop(2, len_x - 2, inner, 0)
+        for chunk in range(CHUNKS):
+            edges(chunk)
+            if chunk == CHUNKS - 2:
+                lax.fori_loop(2, len_x - 2, inner, 0)
+
+                @pl.when(step == STEPS - 1)
+                def _():
+                    store(0).start()
 
         @pl.when(step < STEPS - 1)
         def _():
@@ -379,10 +428,8 @@
         return carry
 
     lax.fori_loop(0, STEPS, step_body, 0)
-    store = pltpu.make_async_copy(
-        buf.at[STEPS % 2, :, pl.ds(2, len_x), pl.ds(PAD, len_y), :], out_ref, load_sem
-    )
-    store.start()
+    store(1).start()
+    store(2).start()
     lane_o = lax.broadcasted_iota(jnp.int32, (1, owned), 1)
     result = jnp.zeros((1, owned), jnp.float32)
     for r in range(owned):
@@ -390,7 +437,8 @@
         value = jnp.sum(mine_r * integral_ref[...]) + (1.0 - jnp.sum(mine_r)) * state_ref[0, r]
         result = jnp.where(lane_o == r, value, result)
     next_ref[...] = result
-    store.wait()
+    for part in range(3):
+        store(part).wait()
 
 
 def local(
@@ -412,7 +460,7 @@
     wide = -(-max(len_z, turbines) // 128) * 128
     any_spec = pl.BlockSpec(memory_space=pl.ANY)
     vmem = pl.BlockSpec(memory_space=pltpu.VMEM)
-    smem = pl.BlockSpec(memory_space=pltpu.SMEM)
+    hbm = pl.BlockSpec(memory_space=pltpu.HBM)
     f32 = jnp.float32
     dma = pltpu.SemaphoreType.DMA
     out, prof, thrust, following = pl.pallas_call(
@@ -423,7 +471,7 @@
             jax.ShapeDtypeStruct((1, turbines), f32),
             jax.ShapeDtypeStruct((1, owned), f32),
         ),
-        in_specs=[any_spec, vmem, smem, smem, vmem, vmem, vmem, smem],
+        in_specs=[hbm] * 8,
         out_specs=(any_spec, vmem, vmem, vmem),
         scratch_shapes=[
             pltpu.VMEM((2, 3, len_x + 4, len_y + 2 * PAD, len_z), f32),
@@ -447,9 +495,18 @@
             pltpu.SMEM((slots,), f32),
             pltpu.VMEM((owned, turbines), f32),
             pltpu.VMEM((2, 8, len_z), f32),
+            pltpu.VMEM(target_profile.shape, f32),
+            pltpu.SMEM(disc_turbine.shape, jnp.int32),
+            pltpu.SMEM(disc_start.shape, jnp.int32),
+            pltpu.VMEM(disc_weight.shape, f32),
+            pltpu.VMEM((1, turbines), jnp.int32),
+            pltpu.VMEM((1, turbines), jnp.int32),
+            pltpu.SMEM(controller_state.shape, f32),
+            dma((7,)),
+            dma((3,)),
         ],
         compiler_params=pltpu.CompilerParams(
-            collective_id=0, has_side_effects=True, vmem_limit_bytes=48 * 1024 * 1024
+            collective_id=0, has_side_effects=True, vmem_limit_bytes=67_043_328
         ),
     )(
         velocity,

time: 143 us -> 128 us (0.90)
  Pallas kernels: 133 us -> 122 us
  local copies, waits for them, and re-layouts: 9.42 us -> 4.93 us
    pallas_call x1, Pallas kernels: 133 us -> 122 us  [local(): pl.pallas_call(functools.partial(kernel, n_gx, n_gy), out_shape=(jax.Shap...]
    unnamed x20 -> x10, local copies, waits for them, and re-layouts: 9.42 us -> 4.93 us
where the time goes in v2:
time: 128 us; the launch traced here: 127 us
  Pallas kernels  122 us (95%)
  local copies, waits for them, and re-layouts  4.93 us (4%)
    pallas_call x1, Pallas kernels, local(): pl.pallas_call(functools.partial(kernel, n_gx, n_gy), out_shape=(jax.Shap...  122 us
    unnamed x10, local copies, waits for them, and re-layouts  4.93 us

profile of v2, /device:TPU:0, one launch (start us, length us, event | category | flops | bytes accessed | tf_op | source)
XLA Modules:
  0.0 127.5 jit_solution(16737210495876373865)
XLA Ops:
  0.6 121.9 %shard_map.111 = (f32[3,8,64,384]{3,2,1,0:T(8,128)}, f32[4,384]{1,0:T(4,128)}, f32[1,100]{1,0:T(1,128)}, f32[1,4]{1,0:T(1,128)}) custom-call(f32[3,8,64,384]{3,2,1,0:T(8,128)} %vel_ref.1, f32[2,384]{1,0:T(2,128)} %target_in.1, s32[1,4]{1,0:T(1,128)} %turbine_in.1, s32[3,1,4]{2,1,0:T(1,128)} %start_in.1, f32[1,4,16,128]{3,2,1,0:T(8,128)} %weight_in.1, ...), custom_call_target="tpu_custom_call" | custom-call | tf_op jit(solution)/shard_map/pallas_call | solution.py:466
  122.5 0.0 copy-start
  122.5 0.0 copy-start.2
  122.6 0.0 copy-start.1
  122.6 3.3 %copy.16 = f32[3,8,64,384]{3,2,1,0:T(8,128)} copy(f32[3,8,64,384]{3,2,1,0:T(8,128)} %get-tuple-element.16) | data formatting | bytes 4718592
  125.9 0.0 copy-done
  125.9 0.6 copy.17
  126.5 0.0 copy-done.2
  126.5 0.5 copy.18
  127.0 0.0 copy-done.1
  127.0 0.5 copy.19
Async XLA Ops:
  122.5 3.3 %copy-start = (f32[4,384]{1,0:T(4,128)S(1)}, f32[4,384]{1,0:T(4,128)}, u32[]{:S(2)}) copy-start(f32[4,384]{1,0:T(4,128)} %get-tuple-element.17) | copy-start | bytes 18436
  122.5 3.9 %copy-start.2 = (f32[1,100]{1,0:T(1,128)S(1)}, f32[1,100]{1,0:T(1,128)}, u32[]{:S(2)}) copy-start(f32[1,100]{1,0:T(1,128)} %get-tuple-element.10) | copy-start | bytes 1204
  122.6 4.4 %copy-start.1 = (f32[1,4]{1,0:T(1,128)S(1)}, f32[1,4]{1,0:T(1,128)}, u32[]{:S(2)}) copy-start(f32[1,4]{1,0:T(1,128)} %get-tuple-element.19) | copy-start | bytes 52
